TPU v7x, 32 devices: a whole 2x2x4 slice. The times are simulated.
32 devices in a mesh: row: 8 (over z, y), col: 4 (over x, core).
Axes of the slice: x: 2, y: 2, z: 4, core: 2. Of those that a mesh axis runs over, the one named last changes fastest.
Arguments:
- act_quant: bfloat16 [512, 8192], P('row', 'col'), may hold values from -127 to 127, as said below
- act_scale: float32 [512], replicated, may hold values from 0.004 to 0.04
- gate_up_quant: bfloat16 [2, 8192, 29568], P(None, 'col', 'row'), may hold values from -127 to 127, as said below
- gate_up_scale: float32 [2, 29568], P(None, 'row'), may hold values from 5e-05 to 0.0005
- down_quant: bfloat16 [29568, 8192], P('row', 'col'), may hold values from -127 to 127, as said below
- down_scale: float32 [8192], P('col'), may hold values from 3e-05 to 0.0003
Outputs:
- mixed_out: bfloat16 [512, 8192], P('row', 'col')
Inputs may be any that keep to these rules, and one draw needn't show every extreme that they name: `act_quant`: whole numbers. `gate_up_quant`: whole numbers. `down_quant`: whole numbers.
All inputs are finite; a program needn't handle non-finite values.
Results may differ from a plain program's by a relative error of at most 0.005.
Values may be sent and summed in bfloat16 or wider, within the bound.
A program may use at most 128 MiB of HBM per device.

v0:
```python
import functools

import jax
import jax.numpy as jnp
from jax import lax
from jax.experimental import pallas as pl
from jax.experimental.pallas import tpu as pltpu
from jax.sharding import PartitionSpec as P

MESH = pl.DeviceIdType.MESH
SUB = 16
TILE = 512
F32, BF16 = jnp.float32, jnp.bfloat16


def for_tiles(width, fn):
    full = width // TILE
    if full:
        def step(j, carry):
            fn(pl.multiple_of(j * TILE, TILE), TILE)
            return carry
        lax.fori_loop(0, full, step, 0)
    if width % TILE:
        fn(full * TILE, width % TILE)


def kernel(K, Rz, Ry, X, act, act_scale, gu_hbm, gu_scale, down_hbm, down_scale, out,
           wgu, wdn, acts, keep, dsend, drecv, xsend, xrecv, hid, opart, ysend, yrecv, zsend, zrecv, zown,
           w_sem, az_s, az_r, ay_s, ay_r, d_s, d_r, x_s, x_r, h_s, h_r, f_s, f_r, y_s, y_r, z_s, z_r, credit):
    R, C = Rz * Ry, X * 2
    Fl, Dl = wgu.shape[1], wgu.shape[2]
    half = R * SUB // 2
    own = R * SUB // C
    nb = R // C
    row, col = lax.axis_index("row"), lax.axis_index("col")
    z, y = row // Ry, lax.rem(row, Ry)
    x, core = col // 2, lax.rem(col, 2)
    pos = core * X + x
    partner = {"row": row, "col": x * 2 + 1 - core}

    def zdev(dz):
        return {"row": lax.rem(z + dz, Rz) * Ry + y, "col": col}

    def ydev(dy):
        return {"row": z * Ry + lax.rem(y + dy, Ry), "col": col}

    def xdev(dx):
        return {"row": row, "col": lax.rem(x + dx, X) * 2 + core}

    def remote(src, dst, s, r, dev):
        return pltpu.make_async_remote_copy(src_ref=src, dst_ref=dst, send_sem=s, recv_sem=r,
                                            device_id=dev, device_id_type=MESH)

    wcopies = []
    cut = Fl // 2 // SUB * SUB
    for g in range(2):
        for h, part in enumerate((pl.ds(0, cut), pl.ds(cut, Fl - cut))):
            wcopies.append(pltpu.make_async_copy(gu_hbm.at[g, part], wgu.at[g, part], w_sem.at[g * 2 + h]))
    dcopy = pltpu.make_async_copy(down_hbm, wdn, w_sem.at[4])
    for c in wcopies:
        c.start()
    dcopy.start()

    barrier = pltpu.get_barrier_semaphore()
    peers = ([zdev(d) for d in range(1, Rz)] + [ydev(d) for d in range(1, Ry)]
             + [xdev(d) for d in range(1, X)] + [partner])
    for p in peers:
        pl.semaphore_signal(barrier, inc=1, device_id=p, device_id_type=MESH)
    pl.semaphore_wait(barrier, len(peers))

    az = [[remote(act.at[pl.ds(k * SUB, SUB)], acts.at[k, z, y], az_s.at[k, d - 1], az_r.at[k, d - 1], zdev(d))
           for d in range(1, Rz)] for k in range(K)]
    ay = [[remote(acts.at[k, :, y], acts.at[k, :, y], ay_s.at[k, d - 1], ay_r.at[k, d - 1], ydev(d))
           for d in range(1, Ry)] for k in range(K)]
    for k in range(K):
        for c in az[k]:
            c.start()
    for k in range(K):
        acts[k, z, y] = act[k * SUB:(k + 1) * SUB, :]

    def forward_acts(k):
        for c in az[k]:
            c.wait_recv()
        for c in ay[k]:
            c.start()

    dd = [[remote(dsend.at[g], drecv.at[g], d_s.at[k, g], d_r.at[k, g], partner) for g in range(2)] for k in range(K)]
    xx = [[remote(xsend.at[k % 2, d - 1], xrecv.at[k, d - 1], x_s.at[k, d - 1], x_r.at[k, d - 1], xdev(d))
           for d in range(1, X)] for k in range(K)]
    hh = [[remote(hid.at[k, pos], hid.at[k, pos], h_s.at[k, d - 1], h_r.at[k, d - 1], xdev(d))
           for d in range(1, X)] for k in range(K)]
    ff = [remote(hid.at[k, pl.ds(core * X, X)], hid.at[k, pl.ds(core * X, X)], f_s.at[k], f_r.at[k], partner)
          for k in range(K)]
    yy = [[remote(ysend.at[k % 2, d - 1], yrecv.at[k, d - 1], y_s.at[k, d - 1], y_r.at[k, d - 1], ydev(d))
           for d in range(1, Ry)] for k in range(K)]
    zz = [[remote(zsend.at[k % 2, d - 1], zrecv.at[k, d - 1], z_s.at[k, d - 1], z_r.at[k, d - 1], zdev(d))
           for d in range(1, Rz)] for k in range(K)]

    def stage_g(k):
        for c in ay[k]:
            c.wait_recv()
        if k + 1 < K:
            forward_acts(k + 1)
        if k == 0:
            for c in wcopies:
                c.wait()
        else:
            for c in dd[k - 1]:
                c.wait_send()
        blocks = Rz // 2
        for g in range(2):
            def tile(start, size, g=g):
                lhs = jnp.concatenate([
                    acts[k, pl.ds(core * blocks, blocks)].reshape(half, Dl),
                    acts[k, pl.ds((1 - core) * blocks, blocks)].reshape(half, Dl)], axis=0)
                r = lax.dot_general(lhs, wgu[g, pl.ds(start, size), :], (((1,), (1,)), ((), ())),
                                    preferred_element_type=F32)
                keep[k % 2, g, :, pl.ds(start, size)] = r[:half]
                dsend[g, :, pl.ds(start, size)] = r[half:]
            for_tiles(Fl, tile)
            if k >= 1 and g == 0:
                pl.semaphore_wait(credit, 1)
            dd[k][g].start()

    def stage_x(k):
        for c in dd[k]:
            c.wait_recv()
        if k >= 2:
            for c in xx[k - 2]:
                c.wait_send()
        for d in range(1, X):
            rows = pl.ds(pl.multiple_of(lax.rem(x + d, X) * own, own), own)
            for g in range(2):
                def tile(start, size, g=g, rows=rows, d=d):
                    cols = pl.ds(start, size)
                    xsend[k % 2, d - 1, g, :, cols] = (keep[k % 2, g, rows, cols] + drecv[g, rows, cols]).astype(BF16)
                for_tiles(Fl, tile)
            xx[k][d - 1].start()
        rows = pl.ds(pl.multiple_of(x * own, own), own)
        for g in range(2):
            def tile(start, size, g=g):
                cols = pl.ds(start, size)
                keep[k % 2, g, rows, cols] = keep[k % 2, g, rows, cols] + drecv[g, rows, cols]
            for_tiles(Fl, tile)
        if k + 1 < K:
            pl.semaphore_signal(credit, inc=1, device_id=partner, device_id_type=MESH)

    def stage_s(k):
        for c in xx[k]:
            c.wait_recv()
        rows = pl.ds(pl.multiple_of(x * own, own), own)
        scale = jnp.concatenate([act_scale[pos * nb + i, k] for i in range(nb)], axis=0)

        def tile(start, size):
            cols = pl.ds(start, size)
            vals = []
            for g in range(2):
                v = keep[k % 2, g, rows, cols]
                for d in range(1, X):
                    v = v + xrecv[k, d - 1, g, :, cols].astype(F32)
                vals.append(v * scale * gu_scale[g:g + 1, cols])
            hid[k, pos, :, cols] = (vals[0] / (1.0 + jnp.exp(-vals[0])) * vals[1]).astype(BF16)
        for_tiles(Fl, tile)
        for c in hh[k]:
            c.start()

    def stage_d(k):
        for c in hh[k]:
            c.wait_recv()
        ff[k].start()
        if k == 0:
            dcopy.wait()
        if k >= 2:
            for c in yy[k - 2]:
                c.wait_send()
        ff[k].wait_recv()

        def tile(start, size):
            r = jnp.dot(hid[k].reshape(R * SUB, Fl), wdn[:, pl.ds(start, size)], preferred_element_type=F32)
            opart[:, :, :, pl.ds(start, size)] = r.reshape(Rz, Ry, SUB, size)
        for_tiles(Dl, tile)
        for d in range(1, Ry):
            ysend[k % 2, d - 1] = opart[:, lax.rem(y + d, Ry)].astype(BF16)
            yy[k][d - 1].start()

    def stage_y(k):
        for c in yy[k]:
            c.wait_recv()
        if k >= 2:
            for c in zz[k - 2]:
                c.wait_send()
        for d in range(1, Rz + 1):
            zt = lax.rem(z + d, Rz)
            v = opart[zt, y]
            for e in range(1, Ry):
                v = v + yrecv[k, e - 1, zt].astype(F32)
            if d < Rz:
                zsend[k % 2, d - 1] = v.astype(BF16)
                zz[k][d - 1].start()
            else:
                zown[k] = v

    def stage_z(k):
        for c in zz[k]:
            c.wait_recv()
        v = zown[k]
        for d in range(1, Rz):
            v = v + zrecv[k, d - 1].astype(F32)
        out[k * SUB:(k + 1) * SUB, :] = (v * down_scale[...]).astype(BF16)

    forward_acts(0)
    for it in range(K + 3):
        if it < K:
            stage_g(it)
        if 0 <= it - 1 < K:
            stage_s(it - 1)
        if 0 <= it - 3 < K:
            stage_y(it - 3)
        if 0 <= it - 2 < K:
            stage_d(it - 2)
        if it < K:
            stage_x(it)
    for k in range(K):
        stage_z(k)

    for k in range(K):
        for c in az[k] + ay[k] + hh[k] + [ff[k]]:
            c.wait_send()
    for c in dd[K - 1]:
        c.wait_send()
    for k in range(max(K - 2, 0), K):
        for c in xx[k] + yy[k] + zz[k]:
            c.wait_send()


def solution(mesh):
    R, C = mesh.shape["row"], mesh.shape["col"]
    X = C // 2
    Ry = max(d for d in range(1, R + 1) if R % d == 0 and d * d <= R)
    Rz = R // Ry

    def body(act, act_scale, gu, gu_scale, down, down_scale):
        tpr, Dl = act.shape
        Fl = gu.shape[2]
        K = tpr // SUB
        T = R * SUB
        own = T // C
        vmem = pl.BlockSpec(memory_space=pltpu.VMEM)
        hbm = pl.BlockSpec(memory_space=pl.ANY)
        dma = pltpu.SemaphoreType.DMA
        scratch = [
            pltpu.VMEM((2, Fl, Dl), BF16),
            pltpu.VMEM((Fl, Dl), BF16),
            pltpu.VMEM((K, Rz, Ry, SUB, Dl), BF16),
            pltpu.VMEM((2, 2, T // 2, Fl), F32),
            pltpu.VMEM((2, T // 2, Fl), F32),
            pltpu.VMEM((2, T // 2, Fl), F32),
            pltpu.VMEM((2, X - 1, 2, own, Fl), BF16),
            pltpu.VMEM((K, X - 1, 2, own, Fl), BF16),
            pltpu.VMEM((K, C, own, Fl), BF16),
            pltpu.VMEM((Rz, Ry, SUB, Dl), F32),
            pltpu.VMEM((2, Ry - 1, Rz, SUB, Dl), BF16),
            pltpu.VMEM((K, Ry - 1, Rz, SUB, Dl), BF16),
            pltpu.VMEM((2, Rz - 1, SUB, Dl), BF16),
            pltpu.VMEM((K, Rz - 1, SUB, Dl), BF16),
            pltpu.VMEM((K, SUB, Dl), F32),
            dma((5,)),
            dma((K, Rz - 1)), dma((K, Rz - 1)),
            dma((K, Ry - 1)), dma((K, Ry - 1)),
            dma((K, 2)), dma((K, 2)),
            dma((K, X - 1)), dma((K, X - 1)),
            dma((K, X - 1)), dma((K, X - 1)),
            dma((K,)), dma((K,)),
            dma((K, Ry - 1)), dma((K, Ry - 1)),
            dma((K, Rz - 1)), dma((K, Rz - 1)),
            pltpu.SemaphoreType.REGULAR,
        ]
        return pl.pallas_call(
            functools.partial(kernel, K, Rz, Ry, X),
            out_shape=jax.ShapeDtypeStruct((tpr, Dl), BF16),
            in_specs=[vmem, vmem, hbm, vmem, hbm, vmem],
            out_specs=vmem,
            scratch_shapes=scratch,
            compiler_params=pltpu.CompilerParams(
                collective_id=0, has_side_effects=True, vmem_limit_bytes=67043328
            ),
        )(act, act_scale.reshape(R, K, SUB, 1), jnp.swapaxes(gu, 1, 2), gu_scale, down, down_scale.reshape(1, Dl))

    in_specs = (P("row", "col"), P(), P(None, "col", "row"), P(None, "row"), P("row", "col"), P("col"))
    return jax.shard_map(body, mesh=mesh, in_specs=in_specs, out_specs=P("row", "col"), check_vma=False)
```

profile of v0, /device:TPU:0, one launch (start us, length us, event | category | flops | bytes accessed | tf_op | source)
XLA Modules:
  0.0 142.3 jit_solution(12982805156307165164)
XLA Ops:
  0.0 1.6 %reshape.8.act_scale = f32[8,4,16,1]{3,2,1,0:T(8,128)} reshape(f32[512]{0:T(512)} %param.7) | data formatting | bytes 4096 | tf_op jit(solution)/shard_map/reshape | solution.py:287
  1.6 139.1 %shard_map.64 = bf16[64,2048]{1,0:T(8,128)(2,1)} custom-call(bf16[64,2048]{1,0:T(8,128)(2,1)} %act.1, f32[8,4,16,1]{3,2,1,0:T(8,128)} %reshape.8.act_scale, bf16[2,3696,2048]{2,1,0:T(8,128)(2,1)} %bitcast.2, f32[2,3696]{1,0:T(2,128)} %gu_scale.1, bf16[3696,2048]{1,0:T(8,128)(2,1)} %down_hbm.1, f32[1,2048]{1,0:T(1,128)} %bitcast.3), custom_call_target="tpu_custom_call" | custom-call | tf_op jit(solution)/shard_map/pallas_call | solution.py:278
  140.7 1.7 %copy.9 = bf16[64,2048]{1,0:T(8,128)(2,1)} copy(bf16[64,2048]{1,0:T(8,128)(2,1)} %shard_map.64) | data formatting | bytes 524288
where the time goes:
time: 143 us; the launch traced here: 142 us
  Pallas kernels  139 us (97%)
  local copies, waits for them, and re-layouts  3.26 us (2%)
    pallas_call x1, Pallas kernels, body(): pl.pallas_call(functools.partial(kernel, K, Rz, Ry, X), out_shape=jax.Sha...  139 us

commit v1 on v0

v1 whole, which is shorter than its diff:
```python
import functools

import jax
import jax.numpy as jnp
from jax import lax
from jax.experimental import pallas as pl
from jax.experimental.pallas import tpu as pltpu
from jax.sharding import PartitionSpec as P

MESH = pl.DeviceIdType.MESH
SMALL, LARGE = 8, 16
RING = 3
FIRST = (512, 1024)
GTILE = 1280
DTILE = 1024
VTILE = 512
TTILE = 512
F32, BF16 = jnp.float32, jnp.bfloat16
sc = jax.named_scope


def pieces(width, size):
    return [(s, min(size, width - s)) for s in range(0, width, size)]


def blocks_of(width):
    out, start = [], 0
    for size in FIRST:
        if start + size < width:
            out.append((start, size))
            start += size
    return out + [(start + s, w) for s, w in pieces(width - start, GTILE)]


def chunks_of(tokens):
    if tokens % LARGE or tokens < 2 * LARGE:
        return [SMALL] * (tokens // SMALL)
    return [LARGE] * (tokens // LARGE - 1) + [SMALL] * 2


def hop(v, d, n):
    if n & (n - 1):
        return lax.rem(v + d, n)
    r, bit = 0, 1
    while bit < n:
        b = lax.rem(v // bit, 2)
        r = r + bit * ((1 - b) if d & bit else b)
        bit *= 2
    return r


def back(v, d, n):
    return lax.rem(v + n - d, n) if n & (n - 1) else hop(v, d, n)


def for_tiles(start, width, fn, size=VTILE):
    full = width // size
    if full:
        def step(j, carry):
            fn(pl.ds(pl.multiple_of(start + j * size, 128), size))
            return carry
        lax.fori_loop(0, full, step, 0)
    if width % size:
        fn(pl.ds(start + full * size, width % size))


def kernel(ns, Rz, Ry, X, act, act_scale, gu_hbm, gu_scale, down_hbm, down_scale, out, *scratch):
    K = len(ns)
    it_ = iter(scratch)
    take = lambda: next(it_)
    wt, wdn, keep, dsend, drecv, xsend, opart, ysend, zsend, packed = (take() for _ in range(10))
    acts = [take() for _ in ns]
    xrecv = [take() for _ in range(RING)]
    hid = [take() for _ in range(RING)]
    yrecv = [take() for _ in ns]
    zrecv = [take() for _ in ns]
    zown = [take() for _ in ns]
    (w_sem, az_s, az_r, ay_s, ay_r, d_s, d_r, x_s, x_r, h_s, h_r, p_s, p_r, f_s, f_r,
     y_s, y_r, z_s, z_r, credit) = (take() for _ in range(20))

    R, C = Rz * Ry, X * 2
    _, Dl, Fl = wt.shape
    tpr = act.shape[0]
    tok = act_scale.shape[1]
    offs = [sum(ns[:k]) for k in range(K)]
    fblk = blocks_of(Fl)
    NB = len(fblk)
    dblk = pieces(Dl, DTILE)
    nb = R // C
    row, col = lax.axis_index("row"), lax.axis_index("col")
    z, y = row // Ry, lax.rem(row, Ry)
    x, core = col // 2, lax.rem(col, 2)
    pos = core * X + x
    partner = {"row": row, "col": x * 2 + 1 - core}

    def zdev(d):
        return {"row": hop(z, d, Rz) * Ry + y, "col": col}

    def ydev(d):
        return {"row": z * Ry + hop(y, d, Ry), "col": col}

    def xdev(d):
        return {"row": row, "col": hop(x, d, X) * 2 + core}

    def remote(src, dst, s, r, dev):
        return pltpu.make_async_remote_copy(src_ref=src, dst_ref=dst, send_sem=s, recv_sem=r,
                                            device_id=dev, device_id_type=MESH)

    nfull = Fl // TTILE
    tail = Fl - nfull * TTILE

    def wrows(i, size=TTILE):
        return pl.ds(pl.multiple_of(i * TTILE, TTILE) if not isinstance(i, int) else i * TTILE, size)

    def wcopy(g, i, size=TTILE):
        src = gu_hbm.at[g] if g < 2 else down_hbm
        return pltpu.make_async_copy(src.at[wrows(i, size)], wdn.at[wrows(i, size)], w_sem.at[i])

    for i in range(nfull):
        wcopy(0, i).start()
    if tail:
        wcopy(0, nfull, tail).start()

    barrier = pltpu.get_barrier_semaphore()
    peers = ([zdev(d) for d in range(1, Rz)] + [ydev(d) for d in range(1, Ry)]
             + [xdev(d) for d in range(1, X)] + [partner])
    for p in peers:
        pl.semaphore_signal(barrier, inc=1, device_id=p, device_id_type=MESH)

    def turn(g, i, size):
        wcopy(g, i, size).wait()
        half = Dl // 2
        cols = wrows(i, size)

        def part(c, carry):
            rows = pl.ds(pl.multiple_of(c * half, half), half)
            wt[g, rows, cols] = wdn[wrows(i, size), rows].T
            return carry
        lax.fori_loop(0, 2, part, 0)
        wcopy(g + 1, i, size).start()

    def turns(g, lo, hi):
        def step(i, carry):
            turn(g, i, TTILE)
            return carry
        with sc(f"T{g}_{lo}"):
            if hi > lo:
                lax.fori_loop(lo, min(hi, nfull), step, 0)
            if hi > nfull and tail:
                turn(g, nfull, tail)

    with sc("barrier"):
        pl.semaphore_wait(barrier, len(peers))

    az = [[remote(act.at[pl.ds(offs[k], n)], acts[k].at[y, z], az_s.at[k, d - 1], az_r.at[k, d - 1], zdev(d))
           for d in range(1, Rz)] for k, n in enumerate(ns)]
    ay = [[[remote(act.at[pl.ds(offs[k], n)] if d == 0 else acts[k].at[y, back(z, d, Rz)],
                   acts[k].at[y, z if d == 0 else back(z, d, Rz)],
                   ay_s.at[k, d, e - 1], ay_r.at[k, d, e - 1], ydev(e))
            for e in range(1, Ry)] for d in range(Rz)] for k, n in enumerate(ns)]

    def gather(k):
        for c in az[k]:
            c.start()
        for c in ay[k][0]:
            c.start()
        acts[k][y, z] = act[offs[k]:offs[k] + ns[k], :]

    def forward(k, d):
        with sc(f"w_az{k}_{d}"):
            az[k][d - 1].wait_recv()
        for c in ay[k][d]:
            c.start()

    gather(0)

    T = [R * n for n in ns]
    own = [t // C for t in T]
    cols_of = [pl.ds(s, w) for s, w in fblk]
    dd = [[remote(dsend.at[:, pl.ds(0, T[k] // 2), c], drecv.at[:, pl.ds(0, T[k] // 2), c],
                  d_s.at[b], d_r.at[b], partner) for b, c in enumerate(cols_of)] for k in range(K)]
    xx = [[[remote(xsend.at[k % 2, d - 1, :, pl.ds(0, own[k]), c], xrecv[k % RING].at[d - 1, :, pl.ds(0, own[k]), c],
                   x_s.at[k % 2, b, d - 1], x_r.at[k % RING, b, d - 1], xdev(d)) for d in range(1, X)]
           for b, c in enumerate(cols_of)] for k in range(K)]
    hh = [[[remote(hid[k % RING].at[pos, pl.ds(0, own[k]), c], hid[k % RING].at[pos, pl.ds(0, own[k]), c],
                   h_s.at[k % RING, b, d - 1], h_r.at[k % RING, b, d - 1], xdev(d)) for d in range(1, X)]
           for b, c in enumerate(cols_of)] for k in range(K)]
    hp = [[remote(hid[k % RING].at[pos, pl.ds(0, own[k]), c], hid[k % RING].at[pos, pl.ds(0, own[k]), c], p_s.at[k % RING, b], p_r.at[k % RING, b], partner)
           for b, c in enumerate(cols_of)] for k in range(K)]
    ff = [[[remote(hid[k % RING].at[core * X + back(x, d, X), pl.ds(0, own[k]), c], hid[k % RING].at[core * X + back(x, d, X), pl.ds(0, own[k]), c],
                   f_s.at[k % 2, b, d - 1], f_r.at[k % RING, b, d - 1], partner) for d in range(1, X)]
           for b, c in enumerate(cols_of)] for k in range(K)]
    yy = [[[remote(ysend.at[k % 2, d - 1, :, pl.ds(0, ns[k]), pl.ds(s, w)], yrecv[k].at[d - 1, :, :, pl.ds(s, w)],
                   y_s.at[k % 2, t, d - 1], y_r.at[k, t, d - 1], ydev(d)) for d in range(1, Ry)]
           for t, (s, w) in enumerate(dblk)] for k in range(K)]
    zz = [[[remote(zsend.at[k % 2, d - 1, pl.ds(0, ns[k]), pl.ds(s, w)], zrecv[k].at[d - 1, :, pl.ds(s, w)],
                   z_s.at[k % 2, t, d - 1], z_r.at[k, t, d - 1], zdev(d)) for d in range(1, Rz)]
           for t, (s, w) in enumerate(dblk)] for k in range(K)]

    def stage_g(k, b):
        if b == 0:
            with sc(f"w_ay{k}"):
                for d in range(Rz):
                    for c in ay[k][d]:
                        c.wait_recv()
        if k >= 1:
            dd[k - 1][b].wait_send()
        hy, half = Ry // 2, T[k] // 2
        cols = cols_of[b]
        repack = ns[k] < LARGE

        def operand():
            return jnp.concatenate([acts[k][pl.ds(core * hy, hy)].reshape(half, Dl),
                                    acts[k][pl.ds((1 - core) * hy, hy)].reshape(half, Dl)], axis=0)
        if repack and b == 0:
            with sc(f"pack{k}"):
                packed[...] = operand()

        def one(g, carry):
            lhs = jnp.concatenate([packed[...]] * 2, axis=0) if repack else operand()
            r = jnp.dot(lhs, wt[g, :, cols], preferred_element_type=F32)
            keep[k % 2, g, pl.ds(0, half), cols] = r[:half]
            dsend[g, pl.ds(0, half), cols] = r[half:T[k]]
            return carry
        with sc(f"G{k}_{b}"):
            lax.fori_loop(0, 2, one, 0)
        if k >= 1:
            pl.semaphore_wait(credit, 1)
        dd[k][b].start()

    def stage_x(k, b):
        with sc(f"w_dd{k}_{b}"):
            dd[k][b].wait_recv()
        if k >= 2:
            for c in xx[k - 2][b]:
                c.wait_send()
        o = own[k]
        for d in range(1, X):
            rows = pl.ds(pl.multiple_of(hop(x, d, X) * o, o), o)
            for g in range(2):
                def tile(cols, g=g, rows=rows, d=d):
                    xsend[k % 2, d - 1, g, pl.ds(0, o), cols] = (
                        keep[k % 2, g, rows, cols] + drecv[g, rows, cols]).astype(BF16)
                for_tiles(*fblk[b], tile)
            xx[k][b][d - 1].start()
        rows = pl.ds(pl.multiple_of(x * o, o), o)
        for g in range(2):
            def tile(cols, g=g):
                keep[k % 2, g, rows, cols] = keep[k % 2, g, rows, cols] + drecv[g, rows, cols]
            for_tiles(*fblk[b], tile)
        if k + 1 < K:
            pl.semaphore_signal(credit, inc=1, device_id=partner, device_id_type=MESH)

    def stage_s(k):
        o, n = own[k], ns[k]
        scales = []
        for i in range(nb):
            blk = pos * nb + i
            first = (lax.rem(blk, Rz) * Ry + blk // Rz) * tpr + offs[k]
            want = first + lax.broadcasted_iota(jnp.int32, (n, tok), 0)
            hit = lax.broadcasted_iota(jnp.int32, (n, tok), 1) == want
            scales.append(jnp.sum(jnp.where(hit, act_scale[...], 0.0), axis=1, keepdims=True))
        scale = jnp.concatenate(scales, axis=0)
        rows = pl.ds(pl.multiple_of(x * o, o), o)
        for b in range(NB):
            with sc(f"w_xx{k}_{b}"):
                for c in xx[k][b]:
                    c.wait_recv()

            def tile(cols):
                vals = []
                for g in range(2):
                    v = keep[k % 2, g, rows, cols]
                    for d in range(1, X):
                        v = v + xrecv[k % RING][d - 1, g, pl.ds(0, o), cols].astype(F32)
                    vals.append(v * scale * gu_scale[g:g + 1, cols])
                hid[k % RING][pos, pl.ds(0, o), cols] = (vals[0] / (1.0 + jnp.exp(-vals[0])) * vals[1]).astype(BF16)
            with sc(f"S{k}_{b}"):
                for_tiles(*fblk[b], tile)
            for c in hh[k][b]:
                c.start()
            hp[k][b].start()

    def stage_h(k):
        for b in range(NB):
            with sc(f"w_hh{k}_{b}"):
                for c in hh[k][b]:
                    c.wait_recv()
            for c in ff[k][b]:
                c.start()

    def ready_d(k):
        if k == 0:
            with sc("w_down"):
                for i in range(nfull):
                    wcopy(2, i).wait()
                if tail:
                    wcopy(2, nfull, tail).wait()
        if k >= 2:
            for t in range(len(dblk)):
                for c in yy[k - 2][t]:
                    c.wait_send()
        with sc(f"w_ff{k}"):
            for b in range(NB):
                hp[k][b].wait_recv()
                for c in ff[k][b]:
                    c.wait_recv()

    def after_d(k):
        for c in sum(ff[k], []):
            c.wait_send()

    def stage_d(k):
        ready_d(k)
        for t in range(len(dblk)):
            down_tile(k, t)
        after_d(k)

    def down_tile(k, t):
        n, per = ns[k], C // Ry
        s, w = dblk[t]
        with sc(f"D{k}_{t}"):
            lhs = [hid[k % RING][pl.ds(hop(y, d, Ry) * per, per), pl.ds(0, own[k])].reshape(T[k] // Ry, Fl)
                   for d in range(Ry)]
            lhs = jnp.concatenate(lhs * (LARGE // n), axis=0)
            r = jnp.dot(lhs, wdn[:, pl.ds(s, w)], preferred_element_type=F32)[:T[k]].reshape(Ry, Rz, n, w)
            opart[k % 2, :, pl.ds(0, n), pl.ds(s, w)] = r[0]
            for d in range(1, Ry):
                ysend[k % 2, d - 1, :, pl.ds(0, n), pl.ds(s, w)] = r[d].astype(BF16)
        for c in yy[k][t]:
            c.start()

    def stage_y(k, only=None):
        n = ns[k]
        for t, (s, w) in enumerate(dblk):
            if only is not None and t not in only:
                continue
            with sc(f"w_yy{k}_{t}"):
                for c in yy[k][t]:
                    c.wait_recv()
            if k >= 2:
                for c in zz[k - 2][t]:
                    c.wait_send()
            cols = pl.ds(s, w)
            for d in range(1, Rz + 1):
                zt = hop(z, d, Rz) if d < Rz else z
                v = opart[k % 2, zt, pl.ds(0, n), cols]
                for e in range(1, Ry):
                    v = v + yrecv[k][e - 1, zt, :, cols].astype(F32)
                if d < Rz:
                    zsend[k % 2, d - 1, pl.ds(0, n), cols] = v.astype(BF16)
                    zz[k][t][d - 1].start()
                else:
                    zown[k][:, cols] = v

    def stage_z(k):
        for t, (s, w) in enumerate(dblk):
            with sc(f"w_zz{k}_{t}"):
                for c in zz[k][t]:
                    c.wait_recv()
            cols = pl.ds(s, w)
            v = zown[k][:, cols]
            for d in range(1, Rz):
                v = v + zrecv[k][d - 1, :, cols].astype(F32)
            out[offs[k]:offs[k] + ns[k], cols] = (v * down_scale[:, cols]).astype(BF16)

    order = [(0, i) for i in range(nfull + 1)] + [(1, i) for i in range(nfull + 1)]
    stops = [min((nfull + 1) * (d + 1) // 2, len(order)) for d in range(Rz - 1)] + [len(order)]
    done = 0
    for d, stop in enumerate(stops):
        for g in range(2):
            mine = [i for h, i in order[done:stop] if h == g]
            if mine:
                turns(g, mine[0], mine[-1] + 1)
        done = stop
        if d < Rz - 1:
            forward(0, d + 1)
            if d == min(1, Rz - 2) and K > 1:
                gather(1)

    def settle(k):
        for c in az[k] + sum(ay[k], []) + sum(hh[k], []) + hp[k]:
            c.wait_send()

    last = len(dblk) - 1
    for it in range(K):
        late = it == K - 2 and it >= 2
        for b in range(NB):
            stage_g(it, b)
            if b >= 1 and not late:
                stage_x(it, b - 1)
            if it + 1 < K:
                for d in range(1, Rz):
                    if min(d - 1, NB - 1) == b:
                        forward(it + 1, d)
            if b == min(2, NB - 1) and it + 2 < K:
                gather(it + 2)
        if late:
            stage_s(it - 1)
        for b in range(0 if late else NB - 1, NB):
            stage_x(it, b)
        if it >= 3:
            stage_y(it - 3)
        if it >= 2 and it == K - 1:
            stage_h(it - 2)
            stage_d(it - 2)
        if it >= 1 and not late:
            stage_s(it - 1)
        if it >= 2 and it < K - 1:
            stage_h(it - 2)
            stage_d(it - 2)
        if it >= 3:
            settle(it - 3)
        if it >= 4:
            stage_z(it - 4)
    if K >= 3:
        settle(K - 3)
    if K >= 2:
        for c in sum(xx[K - 2], []):
            c.wait_send()
    stage_s(K - 1)
    if K >= 3:
        stage_y(K - 3, range(last))
    if K >= 2:
        stage_h(K - 2)
    if K >= 3:
        stage_y(K - 3, (last,))
    if K >= 2:
        ready_d(K - 2)
    for t in range(len(dblk)):
        if K >= 2:
            down_tile(K - 2, t)
        if t == 0:
            stage_h(K - 1)
    ready_d(K - 1)
    for t in range(len(dblk)):
        down_tile(K - 1, t)
        if K >= 2:
            stage_y(K - 2, (t,))
    for k in range(max(K - 2, 0), K):
        after_d(k)
        settle(k)
    for c in dd[K - 1] + sum(xx[K - 1], []):
        c.wait_send()
    if K >= 4:
        stage_z(K - 4)
    stage_y(K - 1)
    for k in range(max(K - 2, 0), K):
        for c in sum(yy[k], []):
            c.wait_send()
    for k in range(max(K - 3, 0), K):
        stage_z(k)
    with sc("end"):
        for k in range(max(K - 2, 0), K):
            for c in sum(zz[k], []):
                c.wait_send()


def solution(mesh):
    R, C = mesh.shape["row"], mesh.shape["col"]
    X = C // 2
    Ry = max(d for d in range(1, R + 1) if R % d == 0 and d * d <= R)
    Rz = R // Ry

    def body(act, act_scale, gu, gu_scale, down, down_scale):
        tpr, Dl = act.shape
        Fl = gu.shape[2]
        ns = chunks_of(tpr)
        K, n = len(ns), max(ns)
        T = R * n
        own = T // C
        NB, ND, NT = len(blocks_of(Fl)), len(pieces(Dl, DTILE)), len(pieces(Fl, TTILE))
        vmem = pl.BlockSpec(memory_space=pltpu.VMEM)
        hbm = pl.BlockSpec(memory_space=pl.ANY)
        dma = pltpu.SemaphoreType.DMA
        scratch = [
            pltpu.VMEM((2, Dl, Fl), BF16),
            pltpu.VMEM((Fl, Dl), BF16),
            pltpu.VMEM((2, 2, T // 2, Fl), F32),
            pltpu.VMEM((2, T // 2, Fl), F32),
            pltpu.VMEM((2, T // 2, Fl), F32),
            pltpu.VMEM((2, X - 1, 2, own, Fl), BF16),
            pltpu.VMEM((2, Rz, n, Dl), F32),
            pltpu.VMEM((2, Ry - 1, Rz, n, Dl), BF16),
            pltpu.VMEM((2, Rz - 1, n, Dl), BF16),
            pltpu.VMEM((R * SMALL, Dl), BF16),
            *[pltpu.VMEM((Ry, Rz, m, Dl), BF16) for m in ns],
            *[pltpu.VMEM((X - 1, 2, own, Fl), BF16)] * RING,
            *[pltpu.VMEM((C, own, Fl), BF16)] * RING,
            *[pltpu.VMEM((Ry - 1, Rz, m, Dl), BF16) for m in ns],
            *[pltpu.VMEM((Rz - 1, m, Dl), BF16) for m in ns],
            *[pltpu.VMEM((m, Dl), F32) for m in ns],
            dma((NT,)),
            dma((K, Rz - 1)), dma((K, Rz - 1)),
            dma((K, Rz, Ry - 1)), dma((K, Rz, Ry - 1)),
            dma((NB,)), dma((NB,)),
            dma((2, NB, X - 1)), dma((RING, NB, X - 1)),
            dma((RING, NB, X - 1)), dma((RING, NB, X - 1)),
            dma((RING, NB)), dma((RING, NB)),
            dma((2, NB, X - 1)), dma((RING, NB, X - 1)),
            dma((2, ND, Ry - 1)), dma((K, ND, Ry - 1)),
            dma((2, ND, Rz - 1)), dma((K, ND, Rz - 1)),
            pltpu.SemaphoreType.REGULAR,
        ]
        return pl.pallas_call(
            functools.partial(kernel, ns, Rz, Ry, X),
            out_shape=jax.ShapeDtypeStruct((tpr, Dl), BF16),
            in_specs=[vmem, vmem, hbm, vmem, hbm, vmem],
            out_specs=vmem,
            scratch_shapes=scratch,
            compiler_params=pltpu.CompilerParams(
                collective_id=0, has_side_effects=True, vmem_limit_bytes=67043328
            ),
        )(act, act_scale.reshape(1, -1), jnp.swapaxes(gu, 1, 2), gu_scale, down, down_scale.reshape(1, Dl))

    in_specs = (P("row", "col"), P(), P(None, "col", "row"), P(None, "row"), P("row", "col"), P("col"))
    return jax.shard_map(body, mesh=mesh, in_specs=in_specs, out_specs=P("row", "col"), check_vma=False)
```

time: 143 us -> 102 us (0.71)
  Pallas kernels: 139 us -> 100 us
  local copies, waits for them, and re-layouts: 3.26 us -> 1.67 us
    pallas_call x1, Pallas kernels: 139 us -> 100 us  [body(): pl.pallas_call(functools.partial(kernel, ns, Rz, Ry, X), out_shape=jax.Sh...]
    reshape x1 -> x0, local copies, waits for them, and re-layouts: 1.59 us -> none  [body(): act_scale.reshape(R, K, SUB, 1)]
where the time goes in v1:
time: 102 us
  Pallas kernels  100 us (98%)
  local copies, waits for them, and re-layouts  1.67 us (2%)
    pallas_call x1, Pallas kernels, body(): pl.pallas_call(functools.partial(kernel, ns, Rz, Ry, X), out_shape=jax.Sh...  100 us

profile of v1, /device:TPU:0, one launch (start us, length us, event | category | flops | bytes accessed | tf_op | source)
XLA Modules:
  0.0 102.0 jit_solution(3939193322163680713)
XLA Ops:
  0.0 100.3 %shard_map.64 = bf16[64,2048]{1,0:T(8,128)(2,1)} custom-call(bf16[64,2048]{1,0:T(8,128)(2,1)} %act.1, f32[1,512]{1,0:T(1,128)} %bitcast.5, bf16[2,3696,2048]{2,1,0:T(8,128)(2,1)} %bitcast.3, f32[2,3696]{1,0:T(2,128)} %gu_scale.1, bf16[3696,2048]{1,0:T(8,128)(2,1)} %down_hbm.1, f32[1,2048]{1,0:T(1,128)} %bitcast.4), custom_call_target="tpu_custom_call" | custom-call | tf_op jit(solution)/shard_map/pallas_call | solution.py:505
  100.3 1.7 %copy.8 = bf16[64,2048]{1,0:T(8,128)(2,1)} copy(bf16[64,2048]{1,0:T(8,128)(2,1)} %shard_map.64) | data formatting | bytes 524288

commit v2 on v1

--- a/solution.py
+++ b/solution.py
@@ -12,7 +12,6 @@
 RING = 3
 FIRST = (512, 1024)
 GTILE = 1280
-DTILE = 1024
 VTILE = 512
 TTILE = 512
 F32, BF16 = jnp.float32, jnp.bfloat16
@@ -21,6 +20,10 @@
 
 def pieces(width, size):
     return [(s, min(size, width - s)) for s in range(0, width, size)]
+
+
+def tiles_of(width):
+    return [(0, width // 2), (width // 2, width // 4), (width // 4 * 3, width // 4)]
 
 
 def blocks_of(width):
@@ -64,19 +67,20 @@
         fn(pl.ds(start + full * size, width % size))
 
 
-def kernel(ns, Rz, Ry, X, act, act_scale, gu_hbm, gu_scale, down_hbm, down_scale, out, *scratch):
+def kernel(ns, Rz, Ry, X, act_in, act_scale_in, gu_hbm, gu_scale_in, down_hbm, down_scale_in, out, *scratch):
     K = len(ns)
     it_ = iter(scratch)
     take = lambda: next(it_)
     wt, wdn, keep, dsend, drecv, xsend, opart, ysend, zsend, packed = (take() for _ in range(10))
+    act, act_scale, gu_scale, down_scale, i_sem = (take() for _ in range(5))
     acts = [take() for _ in ns]
     xrecv = [take() for _ in range(RING)]
     hid = [take() for _ in range(RING)]
     yrecv = [take() for _ in ns]
     zrecv = [take() for _ in ns]
     zown = [take() for _ in ns]
-    (w_sem, az_s, az_r, ay_s, ay_r, d_s, d_r, x_s, x_r, h_s, h_r, p_s, p_r, f_s, f_r,
-     y_s, y_r, z_s, z_r, credit) = (take() for _ in range(20))
+    (w_sem, az_s, az_r, ay_s, ay_r, d_s, d_r, x_s, x_r, h_s, h_r, p_s, p_r, f_s,
+     y_s, y_r, z_s, z_r, credit) = (take() for _ in range(19))
 
     R, C = Rz * Ry, X * 2
     _, Dl, Fl = wt.shape
@@ -85,7 +89,7 @@
     offs = [sum(ns[:k]) for k in range(K)]
     fblk = blocks_of(Fl)
     NB = len(fblk)
-    dblk = pieces(Dl, DTILE)
+    dblk = tiles_of(Dl)
     nb = R // C
     row, col = lax.axis_index("row"), lax.axis_index("col")
     z, y = row // Ry, lax.rem(row, Ry)
@@ -116,11 +120,9 @@
         src = gu_hbm.at[g] if g < 2 else down_hbm
         return pltpu.make_async_copy(src.at[wrows(i, size)], wdn.at[wrows(i, size)], w_sem.at[i])
 
-    for i in range(nfull):
-        wcopy(0, i).start()
-    if tail:
-        wcopy(0, nfull, tail).start()
-
+    inputs = [pltpu.make_async_copy(a, b, i_sem.at[i]) for i, (a, b) in enumerate(
+        ((act_in, act), (act_scale_in, act_scale), (gu_scale_in, gu_scale), (down_scale_in, down_scale)))]
+    inputs[0].start()
     barrier = pltpu.get_barrier_semaphore()
     peers = ([zdev(d) for d in range(1, Rz)] + [ydev(d) for d in range(1, Ry)]
              + [xdev(d) for d in range(1, X)] + [partner])
@@ -149,6 +151,14 @@
             if hi > nfull and tail:
                 turn(g, nfull, tail)
 
+    with sc("w_act"):
+        inputs[0].wait()
+    for i in range(nfull):
+        wcopy(0, i).start()
+    if tail:
+        wcopy(0, nfull, tail).start()
+    for c in inputs[1:]:
+        c.start()
     with sc("barrier"):
         pl.semaphore_wait(barrier, len(peers))
 
@@ -156,8 +166,11 @@
            for d in range(1, Rz)] for k, n in enumerate(ns)]
     ay = [[[remote(act.at[pl.ds(offs[k], n)] if d == 0 else acts[k].at[y, back(z, d, Rz)],
                    acts[k].at[y, z if d == 0 else back(z, d, Rz)],
-                   ay_s.at[k, d, e - 1], ay_r.at[k, d, e - 1], ydev(e))
+                   ay_s.at[k, d, e - 1], ay_r.at[k, e - 1], ydev(e))
             for e in range(1, Ry)] for d in range(Rz)] for k, n in enumerate(ns)]
+
+    ay_all = [[remote(acts[k].at[hop(y, e, Ry)], acts[k].at[hop(y, e, Ry)],
+                      ay_s.at[k, 0, e - 1], ay_r.at[k, e - 1], ydev(e)) for e in range(1, Ry)] for k in range(K)]
 
     def gather(k):
         for c in az[k]:
@@ -185,24 +198,23 @@
     hh = [[[remote(hid[k % RING].at[pos, pl.ds(0, own[k]), c], hid[k % RING].at[pos, pl.ds(0, own[k]), c],
                    h_s.at[k % RING, b, d - 1], h_r.at[k % RING, b, d - 1], xdev(d)) for d in range(1, X)]
            for b, c in enumerate(cols_of)] for k in range(K)]
-    hp = [[remote(hid[k % RING].at[pos, pl.ds(0, own[k]), c], hid[k % RING].at[pos, pl.ds(0, own[k]), c], p_s.at[k % RING, b], p_r.at[k % RING, b], partner)
+    hp = [[remote(hid[k % RING].at[pos, pl.ds(0, own[k]), c], hid[k % RING].at[pos, pl.ds(0, own[k]), c], p_s.at[k % RING, b], p_r.at[k % RING], partner)
            for b, c in enumerate(cols_of)] for k in range(K)]
     ff = [[[remote(hid[k % RING].at[core * X + back(x, d, X), pl.ds(0, own[k]), c], hid[k % RING].at[core * X + back(x, d, X), pl.ds(0, own[k]), c],
-                   f_s.at[k % 2, b, d - 1], f_r.at[k % RING, b, d - 1], partner) for d in range(1, X)]
+                   f_s.at[k % 2, b, d - 1], p_r.at[k % RING], partner) for d in range(1, X)]
            for b, c in enumerate(cols_of)] for k in range(K)]
     yy = [[[remote(ysend.at[k % 2, d - 1, :, pl.ds(0, ns[k]), pl.ds(s, w)], yrecv[k].at[d - 1, :, :, pl.ds(s, w)],
                    y_s.at[k % 2, t, d - 1], y_r.at[k, t, d - 1], ydev(d)) for d in range(1, Ry)]
            for t, (s, w) in enumerate(dblk)] for k in range(K)]
     zz = [[[remote(zsend.at[k % 2, d - 1, pl.ds(0, ns[k]), pl.ds(s, w)], zrecv[k].at[d - 1, :, pl.ds(s, w)],
-                   z_s.at[k % 2, t, d - 1], z_r.at[k, t, d - 1], zdev(d)) for d in range(1, Rz)]
+                   z_s.at[k % 2, t, d - 1], z_r.at[k, t], zdev(d)) for d in range(1, Rz)]
            for t, (s, w) in enumerate(dblk)] for k in range(K)]
 
     def stage_g(k, b):
         if b == 0:
             with sc(f"w_ay{k}"):
-                for d in range(Rz):
-                    for c in ay[k][d]:
-                        c.wait_recv()
+                for c in ay_all[k]:
+                    c.wait_recv()
         if k >= 1:
             dd[k - 1][b].wait_send()
         hy, half = Ry // 2, T[k] // 2
@@ -281,8 +293,8 @@
                 c.start()
             hp[k][b].start()
 
-    def stage_h(k):
-        for b in range(NB):
+    def stage_h(k, blocks=None):
+        for b in range(NB) if blocks is None else blocks:
             with sc(f"w_hh{k}_{b}"):
                 for c in hh[k][b]:
                     c.wait_recv()
@@ -301,10 +313,8 @@
                 for c in yy[k - 2][t]:
                     c.wait_send()
         with sc(f"w_ff{k}"):
-            for b in range(NB):
-                hp[k][b].wait_recv()
-                for c in ff[k][b]:
-                    c.wait_recv()
+            theirs = hid[k % RING].at[pl.ds((1 - core) * X, X), pl.ds(0, own[k])]
+            remote(theirs, theirs, p_s.at[k % RING, 0], p_r.at[k % RING], partner).wait_recv()
 
     def after_d(k):
         for c in sum(ff[k], []):
@@ -356,16 +366,16 @@
     def stage_z(k):
         for t, (s, w) in enumerate(dblk):
             with sc(f"w_zz{k}_{t}"):
-                for c in zz[k][t]:
-                    c.wait_recv()
-            cols = pl.ds(s, w)
+                cols = pl.ds(s, w)
+                remote(zrecv[k].at[:, :, cols], zrecv[k].at[:, :, cols], z_s.at[k % 2, t, 0], z_r.at[k, t],
+                       zdev(1)).wait_recv()
             v = zown[k][:, cols]
             for d in range(1, Rz):
                 v = v + zrecv[k][d - 1, :, cols].astype(F32)
             out[offs[k]:offs[k] + ns[k], cols] = (v * down_scale[:, cols]).astype(BF16)
 
     order = [(0, i) for i in range(nfull + 1)] + [(1, i) for i in range(nfull + 1)]
-    stops = [min((nfull + 1) * (d + 1) // 2, len(order)) for d in range(Rz - 1)] + [len(order)]
+    stops = [min(6 + 7 * d // 2, len(order)) for d in range(Rz - 1)] + [len(order)]
     done = 0
     for d, stop in enumerate(stops):
         for g in range(2):
@@ -382,9 +392,10 @@
         for c in az[k] + sum(ay[k], []) + sum(hh[k], []) + hp[k]:
             c.wait_send()
 
-    last = len(dblk) - 1
+    for c in inputs[1:]:
+        c.wait()
     for it in range(K):
-        late = it == K - 2 and it >= 2
+        late = it == 3
         for b in range(NB):
             stage_g(it, b)
             if b >= 1 and not late:
@@ -401,12 +412,9 @@
             stage_x(it, b)
         if it >= 3:
             stage_y(it - 3)
-        if it >= 2 and it == K - 1:
-            stage_h(it - 2)
-            stage_d(it - 2)
         if it >= 1 and not late:
             stage_s(it - 1)
-        if it >= 2 and it < K - 1:
+        if it >= 2:
             stage_h(it - 2)
             stage_d(it - 2)
         if it >= 3:
@@ -419,32 +427,33 @@
         for c in sum(xx[K - 2], []):
             c.wait_send()
     stage_s(K - 1)
+    if K >= 2:
+        stage_h(K - 2, range(NB - 1))
     if K >= 3:
-        stage_y(K - 3, range(last))
+        stage_y(K - 3, (0,))
     if K >= 2:
-        stage_h(K - 2)
-    if K >= 3:
-        stage_y(K - 3, (last,))
-    if K >= 2:
+        stage_h(K - 2, (NB - 1,))
         ready_d(K - 2)
     for t in range(len(dblk)):
         if K >= 2:
             down_tile(K - 2, t)
+        if K >= 3 and t + 1 < len(dblk):
+            stage_y(K - 3, (t + 1,))
         if t == 0:
             stage_h(K - 1)
     ready_d(K - 1)
     for t in range(len(dblk)):
         down_tile(K - 1, t)
-        if K >= 2:
-            stage_y(K - 2, (t,))
+    if K >= 2:
+        stage_y(K - 2)
+    stage_y(K - 1)
+    for c in dd[K - 1] + sum(xx[K - 1], []):
+        c.wait_send()
     for k in range(max(K - 2, 0), K):
         after_d(k)
         settle(k)
-    for c in dd[K - 1] + sum(xx[K - 1], []):
-        c.wait_send()
     if K >= 4:
         stage_z(K - 4)
-    stage_y(K - 1)
     for k in range(max(K - 2, 0), K):
         for c in sum(yy[k], []):
             c.wait_send()
@@ -469,7 +478,7 @@
         K, n = len(ns), max(ns)
         T = R * n
         own = T // C
-        NB, ND, NT = len(blocks_of(Fl)), len(pieces(Dl, DTILE)), len(pieces(Fl, TTILE))
+        NB, ND, NT = len(blocks_of(Fl)), len(tiles_of(Dl)), len(pieces(Fl, TTILE))
         vmem = pl.BlockSpec(memory_space=pltpu.VMEM)
         hbm = pl.BlockSpec(memory_space=pl.ANY)
         dma = pltpu.SemaphoreType.DMA
@@ -484,6 +493,11 @@
             pltpu.VMEM((2, Ry - 1, Rz, n, Dl), BF16),
             pltpu.VMEM((2, Rz - 1, n, Dl), BF16),
             pltpu.VMEM((R * SMALL, Dl), BF16),
+            pltpu.VMEM(act.shape, BF16),
+            pltpu.VMEM((1, act_scale.shape[0]), F32),
+            pltpu.VMEM(gu_scale.shape, F32),
+            pltpu.VMEM((1, Dl), F32),
+            dma((4,)),
             *[pltpu.VMEM((Ry, Rz, m, Dl), BF16) for m in ns],
             *[pltpu.VMEM((X - 1, 2, own, Fl), BF16)] * RING,
             *[pltpu.VMEM((C, own, Fl), BF16)] * RING,
@@ -492,24 +506,24 @@
             *[pltpu.VMEM((m, Dl), F32) for m in ns],
             dma((NT,)),
             dma((K, Rz - 1)), dma((K, Rz - 1)),
-            dma((K, Rz, Ry - 1)), dma((K, Rz, Ry - 1)),
+            dma((K, Rz, Ry - 1)), dma((K, Ry - 1)),
             dma((NB,)), dma((NB,)),
             dma((2, NB, X - 1)), dma((RING, NB, X - 1)),
             dma((RING, NB, X - 1)), dma((RING, NB, X - 1)),
-            dma((RING, NB)), dma((RING, NB)),
-            dma((2, NB, X - 1)), dma((RING, NB, X - 1)),
+            dma((RING, NB)), dma((RING,)),
+            dma((2, NB, X - 1)),
             dma((2, ND, Ry - 1)), dma((K, ND, Ry - 1)),
-            dma((2, ND, Rz - 1)), dma((K, ND, Rz - 1)),
+            dma((2, ND, Rz - 1)), dma((K, ND)),
             pltpu.SemaphoreType.REGULAR,
         ]
         return pl.pallas_call(
             functools.partial(kernel, ns, Rz, Ry, X),
-            out_shape=jax.ShapeDtypeStruct((tpr, Dl), BF16),
-            in_specs=[vmem, vmem, hbm, vmem, hbm, vmem],
+            out_shape=pltpu.VMEM((tpr, Dl), BF16),
+            in_specs=[hbm] * 6,
             out_specs=vmem,
             scratch_shapes=scratch,
             compiler_params=pltpu.CompilerParams(
-                collective_id=0, has_side_effects=True, vmem_limit_bytes=67043328
+                collective_id=0, has_side_effects=True, vmem_limit_bytes=67043328 - 2 * tpr * Dl * 2
             ),
         )(act, act_scale.reshape(1, -1), jnp.swapaxes(gu, 1, 2), gu_scale, down, down_scale.reshape(1, Dl))
 

time: 102 us -> 99.1 us (0.972)
  Pallas kernels: 100 us -> 98.2 us
    pallas_call x1, Pallas kernels: 100 us -> 98.2 us  [body(): pl.pallas_call(functools.partial(kernel, ns, Rz, Ry, X), out_shape=pltpu....]
where the time goes in v2:
time: 99.1 us; the launch traced here: 99 us
  Pallas kernels  98.2 us (99%)
    pallas_call x1, Pallas kernels, body(): pl.pallas_call(functools.partial(kernel, ns, Rz, Ry, X), out_shape=pltpu....  98.2 us

profile of v2, /device:TPU:0, one launch (start us, length us, event | category | flops | bytes accessed | tf_op | source)
XLA Modules:
  0.0 99.0 jit_solution(4645474965649099019)
XLA Ops:
  0.0 98.2 %shard_map.64 = bf16[64,2048]{1,0:T(8,128)(2,1)S(1)} custom-call(bf16[64,2048]{1,0:T(8,128)(2,1)} %act_in.1, f32[1,512]{1,0:T(1,128)} %bitcast.5, bf16[2,3696,2048]{2,1,0:T(8,128)(2,1)} %bitcast.3, f32[2,3696]{1,0:T(2,128)} %gu_scale_in.1, bf16[3696,2048]{1,0:T(8,128)(2,1)} %down_hbm.1, f32[1,2048]{1,0:T(1,128)} %bitcast.4), custom_call_target="tpu_custom_call" | custom-call | tf_op jit(solution)/shard_map/pallas_call | solution.py:519
  98.2 0.7 copy.8

commit v3 on v2

--- a/solution.py
+++ b/solution.py
@@ -375,7 +375,7 @@
             out[offs[k]:offs[k] + ns[k], cols] = (v * down_scale[:, cols]).astype(BF16)
 
     order = [(0, i) for i in range(nfull + 1)] + [(1, i) for i in range(nfull + 1)]
-    stops = [min(6 + 7 * d // 2, len(order)) for d in range(Rz - 1)] + [len(order)]
+    stops = [min(5 + 5 * d // 2, len(order)) for d in range(Rz - 1)] + [len(order)]
     done = 0
     for d, stop in enumerate(stops):
         for g in range(2):

time: 99.1 us -> 98.5 us (level)
  no operation moved by 1% of the time
where the time goes in v3:
time: 98.5 us; the launch traced here: 98.3 us
  Pallas kernels  97.6 us (99%)
    pallas_call x1, Pallas kernels, body(): pl.pallas_call(functools.partial(kernel, ns, Rz, Ry, X), out_shape=pltpu....  97.6 us

profile of v3, /device:TPU:0, one launch (start us, length us, event | category | flops | bytes accessed | tf_op | source)
XLA Modules:
  0.0 98.3 jit_solution(574654228769478904)
XLA Ops:
  0.0 97.6 %shard_map.64 = bf16[64,2048]{1,0:T(8,128)(2,1)S(1)} custom-call(bf16[64,2048]{1,0:T(8,128)(2,1)} %act_in.1, f32[1,512]{1,0:T(1,128)} %bitcast.5, bf16[2,3696,2048]{2,1,0:T(8,128)(2,1)} %bitcast.3, f32[2,3696]{1,0:T(2,128)} %gu_scale_in.1, bf16[3696,2048]{1,0:T(8,128)(2,1)} %down_hbm.1, f32[1,2048]{1,0:T(1,128)} %bitcast.4), custom_call_target="tpu_custom_call" | custom-call | tf_op jit(solution)/shard_map/pallas_call | solution.py:519
  97.6 0.7 copy.8
